TPU v7x, 32 devices: a whole 2x2x4 slice. The times are simulated.
32 devices in a mesh: dp: 8 (over z, y), mp: 4 (over x, core).
Axes of the slice: x: 2, y: 2, z: 4, core: 2. Of those that a mesh axis runs over, the one named last changes fastest.
Arguments:
- tokens: bfloat16 [8192, 4096], P('dp', 'mp'), may hold values from -6 to 6
- right_weight: bfloat16 [64, 64, 64], P('mp', 'dp'), may hold values from -0.75 to 0.75
- left_weight: bfloat16 [64, 64, 64], P('mp', 'dp'), may hold values from -0.75 to 0.75
- cotangent: bfloat16 [8192, 4096], P('dp', 'mp'), may hold values from -0.06591797 to 0.06591797
Outputs:
- activated: bfloat16 [8192, 4096], P('dp', 'mp')
- grad_right: float32 [64, 64, 64], P('mp', 'dp')
- grad_left: float32 [64, 64, 64], P('mp', 'dp')
All inputs are finite; a program needn't handle non-finite values.
Results may differ from a plain program's by a relative error of at most 0.0056.
Values may be sent and summed in bfloat16 or wider, within the bound.
A program may use at most 64 MiB of HBM per device.

v0:
```python
import jax
import jax.numpy as jnp
from jax import lax
from jax.sharding import PartitionSpec as P

NB = 64
BS = 64


def gelu_slope(pre):
    cdf = 0.5 * (1.0 + lax.erf(pre * 0.7071067811865476))
    density = jnp.exp(-0.5 * pre * pre) * 0.3989422804014327
    return cdf + pre * density


def shards(tokens, right_weight, left_weight, cotangent):
    tok_rows = tokens.shape[0]
    groups = lax.axis_size("mp")
    owned = NB // groups
    right_rows, left_rows = (
        lax.all_gather(right_weight, "dp", axis=1, tiled=True),
        lax.all_gather(left_weight, "dp", axis=1, tiled=True),
    )
    xs = tokens.reshape(tok_rows, owned, BS)
    inner = jnp.einsum("tik,ikm->tmi", xs, right_rows, preferred_element_type=jnp.float32)
    inner = inner.astype(jnp.bfloat16).reshape(tok_rows, BS * owned)
    left_four = left_rows.reshape(owned, groups, owned, BS)
    received = lax.all_to_all(inner, "mp", split_axis=1, concat_axis=1, tiled=True)
    rows = received.shape[0]
    mixed = received.reshape(rows, groups, owned, owned)
    pre_rows = jnp.einsum("tpmj,mpjn->tmn", mixed, left_four, preferred_element_type=jnp.float32)
    received, pre = (received, pre_rows)
    mixed = received.reshape(tok_rows, groups, owned, owned)
    activated = (
        jax.nn.gelu(pre, approximate=False).astype(jnp.bfloat16).reshape(tok_rows, owned * BS)
    )
    dpre = (cotangent.reshape(tok_rows, owned, BS).astype(jnp.float32) * gelu_slope(pre)).astype(
        jnp.bfloat16
    )
    part_left = jnp.einsum("tpmj,tmn->mpjn", mixed, dpre, preferred_element_type=jnp.float32)
    part_left = part_left.reshape(owned, NB, BS)
    dmixed = jnp.einsum("tmn,mpjn->tpmj", dpre, left_four, preferred_element_type=jnp.float32)
    dmixed = dmixed.astype(jnp.bfloat16).reshape(tok_rows, groups * owned * owned)
    dinner = lax.all_to_all(dmixed, "mp", split_axis=1, concat_axis=1, tiled=True)
    dinner = dinner.reshape(tok_rows, groups, owned, owned)
    part_right = jnp.einsum("tik,tqmi->ikqm", xs, dinner, preferred_element_type=jnp.float32)
    part_right = part_right.reshape(owned, BS, BS)
    grad_right, grad_left = (
        lax.psum_scatter(part_right, "dp", scatter_dimension=1, tiled=True),
        lax.psum_scatter(part_left, "dp", scatter_dimension=1, tiled=True),
    )
    return (activated, grad_right, grad_left)


def solution(mesh):
    return jax.shard_map(
        shards,
        mesh=mesh,
        in_specs=(P("dp", "mp"), P("mp", "dp", None), P("mp", "dp", None), P("dp", "mp")),
        out_specs=(P("dp", "mp"), P("mp", "dp", None), P("mp", "dp", None)),
        check_vma=False,
    )
```

profile of v0, /device:TPU:0, one launch (start us, length us, event | category | flops | bytes accessed | tf_op | source)
XLA Modules:
  0.0 236.4 jit_solution(14564301819312253097)
XLA Ops:
  7.2 28.6 %all_gather.6 = bf16[16,64,64]{2,1,0:T(8,128)(2,1)S(1)} all-gather(bf16[16,8,64]{2,1,0:T(8,128)(2,1)} %param.5), channel_id=1, replica_groups=mesh['dp'=8,'mp'=4] {'dp'}, dimensions={1}, use_global_device_ids=true | all-gather | bytes 147456 | tf_op jit(solution)/shard_map/all_gather | solution.py:21
  35.7 2.9 %copy.12 = bf16[1024,1024]{0,1:T(8,128)(2,1)S(1)} copy(bf16[1024,1024]{1,0:T(8,128)(2,1)} %param.4) | data formatting | bytes 4194304 | tf_op args[0]
  38.6 0.8 convert_bitcast_fusion.1
  39.3 2.5 %copy.13 = bf16[1024,64,16]{0,2,1:T(8,128)(2,1)} copy(bf16[1024,64,16]{0,1,2:T(8,128)(2,1)S(1)} %convert_bitcast_fusion.1) | data formatting | bytes 4194304 | tf_op jit(solution)/shard_map/convert_element_type | solution.py:26
  41.8 4.5 %all-to-all-start = ((bf16[1024,4,256]{0,2,1:T(8,128)(2,1)}), bf16[1024,4,256]{0,2,1:T(8,128)(2,1)}, u32[]{:S(2)}, u32[]{:S(2)}) async-start(bf16[1024,4,256]{0,2,1:T(8,128)(2,1)} %bitcast.86), calls=%async_computation | async-start | bytes 4194304 | tf_op jit(solution)/shard_map/all_to_all | solution.py:28
  46.3 0.0 copy-start.1
  46.3 4.1 %copy.15 = f32[1024,1024]{0,1:T(8,128)} copy(bf16[1024,1024]{1,0:T(8,128)(2,1)} %param.7) | data formatting | bytes 6291456 | tf_op jit(solution)/shard_map/convert_element_type | solution.py:37
  50.4 0.0 copy-done.1
  50.4 26.4 %all_gather.7 = bf16[16,64,64]{2,1,0:T(8,128)(2,1)S(1)} all-gather(bf16[16,8,64]{2,1,0:T(8,128)(2,1)S(1)} %copy-done.1), channel_id=1, replica_groups=mesh['dp'=8,'mp'=4] {'dp'}, dimensions={1}, use_global_device_ids=true | all-gather | bytes 147456 | tf_op jit(solution)/shard_map/all_gather | solution.py:22
  76.9 0.0 all-to-all-done
  76.9 13.7 %fusion.8 = (bf16[1024,16,64]{0,2,1:T(8,128)(2,1)S(1)}, bf16[1024,16,64]{0,2,1:T(8,128)(2,1)}) fusion(f32[1024,16,64]{0,2,1:T(8,128)} %bitcast.87, bf16[1024,4,16,16]{0,3,2,1:T(8,128)(2,1)} %bitcast.3, bf16[16,4,16,64]{3,2,1,0:T(8,128)(2,1)S(1)} %bitcast.89), kind=kOutput, calls=%fused_computation.10 | convolution fusion | flops 212860928 | bytes 10616832 | tf_op jit(solution)/shard_map/tpmj,mpjn->tmn/dot_general | solution.py:31
  90.5 0.0 copy-start
  90.5 0.7 convert_bitcast_fusion
  91.2 1.5 copy.16
  92.7 0.0 copy-done
  92.7 4.4 %all-to-all-start.1 = ((bf16[1024,4,256]{0,2,1:T(8,128)(2,1)}), bf16[1024,4,256]{0,2,1:T(8,128)(2,1)}, u32[]{:S(2)}, u32[]{:S(2)}) async-start(bf16[1024,4,256]{0,2,1:T(8,128)(2,1)} %bitcast.85), calls=%async_computation.1 | async-start | bytes 4194304 | tf_op jit(solution)/shard_map/all_to_all | solution.py:44
  97.2 0.0 reduce-scatter.5.cloned.1.call-start
  97.2 3.8 %fusion.23 = f32[16,4,16,64]{3,2,1,0:T(8,128)} fusion(bf16[1024,16,64]{0,2,1:T(8,128)(2,1)} %copy-done, bf16[1024,4,16,16]{0,3,2,1:T(8,128)(2,1)} %bitcast.3), kind=kOutput, calls=%fused_computation.34 | convolution fusion | flops 134217728 | bytes 4456448 | tf_op jit(solution)/shard_map/tpmj,tmn->mpjn/dot_general | solution.py:40
  101.0 0.0 reduce-scatter.5.cloned.1.call-update
  101.0 0.0 reduce-scatter.3.cloned.1.call-start
  101.1 21.9 %all-to-all-done.1 = bf16[1024,4,256]{0,2,1:T(8,128)(2,1)} async-done(((bf16[1024,4,256]{0,2,1:T(8,128)(2,1)}), bf16[1024,4,256]{0,2,1:T(8,128)(2,1)}, u32[]{:S(2)}, u32[]{:S(2)}) %all-to-all-start.1) | async-done | bytes 2097184 | tf_op jit(solution)/shard_map/all_to_all | solution.py:44
  122.9 3.1 %fusion.28 = f32[16,4,16,64]{3,2,1,0:T(8,128)S(1)} fusion(bf16[1024,16,64,1]{0,2,3,1:T(8,128)(2,1)S(1)} %bitcast.84, bf16[1024,4,16,16]{0,3,2,1:T(8,128)(2,1)} %bitcast.14), kind=kOutput, calls=%fused_computation.39 | convolution fusion | flops 134217728 | bytes 4456448 | tf_op jit(solution)/shard_map/tik,tqmi->ikqm/dot_general | solution.py:46
  126.0 1.0 copy.18
  127.0 0.0 reduce-scatter.3.cloned.1.call-update
  127.0 4.0 %copy.20 = bf16[1024,1024]{1,0:T(8,128)(2,1)} copy(bf16[1024,1024]{0,1:T(8,128)(2,1)} %bitcast.88) | data formatting | bytes 4194304
  131.0 32.4 %reduce-scatter.5.cloned.1.call-done = f32[16,8,64]{2,1,0:T(8,128)} async-done(((f32[16,64,64]{2,1,0:T(8,128)}), f32[16,8,64]{2,1,0:T(8,128)}) %reduce-scatter.5.cloned.1.call-update) | async-done | bytes 32784 | tf_op jit(solution)/shard_map/reduce_scatter | solution.py:50
  163.4 66.1 %reduce-scatter.3.cloned.1.call-done = f32[16,8,64]{2,1,0:T(8,128)} async-done(((f32[16,64,64]{2,1,0:T(8,128)}), f32[16,8,64]{2,1,0:T(8,128)}) %reduce-scatter.3.cloned.1.call-update) | async-done | bytes 32784 | tf_op jit(solution)/shard_map/reduce_scatter | solution.py:49
Async XLA Ops:
  41.8 35.0 %all-to-all-start = ((bf16[1024,4,256]{0,2,1:T(8,128)(2,1)}), bf16[1024,4,256]{0,2,1:T(8,128)(2,1)}, u32[]{:S(2)}, u32[]{:S(2)}) async-start(bf16[1024,4,256]{0,2,1:T(8,128)(2,1)} %bitcast.86), calls=%async_computation | async-start | bytes 4194304 | tf_op jit(solution)/shard_map/all_to_all | solution.py:28
  46.3 4.1 %copy-start.1 = (bf16[16,8,64]{2,1,0:T(8,128)(2,1)S(1)}, bf16[16,8,64]{2,1,0:T(8,128)(2,1)}, u32[]{:S(2)}) copy-start(bf16[16,8,64]{2,1,0:T(8,128)(2,1)} %param.6) | copy-start | bytes 49156
  90.5 2.2 copy-start
  92.7 30.2 %all-to-all-start.1 = ((bf16[1024,4,256]{0,2,1:T(8,128)(2,1)}), bf16[1024,4,256]{0,2,1:T(8,128)(2,1)}, u32[]{:S(2)}, u32[]{:S(2)}) async-start(bf16[1024,4,256]{0,2,1:T(8,128)(2,1)} %bitcast.85), calls=%async_computation.1 | async-start | bytes 4194304 | tf_op jit(solution)/shard_map/all_to_all | solution.py:44
  97.2 66.2 %reduce-scatter.5.cloned.1.call-start = ((), (), s32[]{:S(2)}) async-start(), calls=%async_computation.5 | async-start | bytes 589824 | tf_op jit(solution)/shard_map/reduce_scatter | solution.py:50
  101.0 128.5 %reduce-scatter.3.cloned.1.call-start = ((), (), s32[]{:S(2)}) async-start(), calls=%async_computation.4 | async-start | bytes 589824 | tf_op jit(solution)/shard_map/reduce_scatter | solution.py:49
Sparse Core Ops, SparseCore 0:
  101.9 61.4 reduce-scatter.4
  167.4 62.1 reduce-scatter.2
where the time goes:
time: 237 us; the launch traced here: 236 us
  waiting for transfers between devices  120 us (51%)
  blocking collectives  55 us (23%)
  matrix products  21.9 us (9%)
  local copies, waits for them, and re-layouts  15.9 us (7%)
  between operations  14.1 us (6%)
  starting transfers between devices  8.99 us (4%)
    reduce_scatter x1, waiting for transfers between devices, shards(): lax.psum_scatter(part_right, 'dp', scatter_dimension=1, tiled=True)  66.1 us
    reduce_scatter x1, waiting for transfers between devices, shards(): lax.psum_scatter(part_left, 'dp', scatter_dimension=1, tiled=True)  32.4 us
    all_gather x1, blocking collectives, shards(): lax.all_gather(right_weight, 'dp', axis=1, tiled=True)  28.6 us
    all_gather x1, blocking collectives, shards(): lax.all_gather(left_weight, 'dp', axis=1, tiled=True)  26.4 us
    all_to_all x1, waiting for transfers between devices, shards(): lax.all_to_all(dmixed, 'mp', split_axis=1, concat_axis=1, tiled=True)  21.9 us
    dot_general x1, matrix products, shards(): jnp.einsum('tpmj,mpjn->tmn', mixed, left_four, preferred_element_type=jnp...  13.7 us
    unnamed x6, local copies, waits for them, and re-layouts  6.83 us
  transfers between devices with their start and end apart: 4, of which 3 were waited for; matrix products, arithmetic and copies ran while one was open for 7% of the time, Pallas kernels for 0%

commit v1 on v0

v1 whole, which is shorter than its diff:
```python
import functools

import jax
import jax.numpy as jnp
from jax import lax
from jax.experimental import pallas as pl
from jax.experimental.pallas import tpu as pltpu
from jax.sharding import PartitionSpec as P

MESH = pl.DeviceIdType.MESH
BF = jnp.bfloat16
F32 = jnp.float32
CHUNKS = 8


def iota(shape, dim):
    return lax.broadcasted_iota(jnp.int32, shape, dim)


def ones_where(cond):
    return jnp.where(cond, 1.0, 0.0).astype(BF)


def dot_nn(a, b):
    return lax.dot_general(a, b, (((1,), (0,)), ((), ())), preferred_element_type=F32)


def dot_nt(a, b):
    return lax.dot_general(a, b, (((1,), (1,)), ((), ())), preferred_element_type=F32)


def dot_tn(a, b):
    return lax.dot_general(a, b, (((0,), (0,)), ((), ())), preferred_element_type=F32)


def join(parts, axis=1):
    return parts[0] if len(parts) == 1 else jnp.concatenate(parts, axis=axis)


class Sizes:
    def __init__(self, n_dp, n_mp, tok_rows, features, width):
        self.dp, self.mp = n_dp, n_mp
        self.tok, self.feat, self.bs = tok_rows, features, width
        self.own = features // width
        self.blocks = self.own * n_mp
        self.rows = width // n_dp
        self.orow = self.own * self.rows
        self.pad = max(self.own, 16)
        self.gs = max(1, 128 // (self.own * self.own))
        self.groups = n_mp // self.gs
        self.ng = self.gs * self.own * self.own
        self.kg = self.gs * features
        self.jg = self.ng // 128
        self.jl = self.own // self.jg
        self.nj = self.ng // self.jg
        self.rh = self.groups * self.nj
        self.fj = self.jl * width
        self.n = n_dp * n_mp
        self.tc = tok_rows // CHUNKS


def kernel(z, x_hbm, cot_hbm, rw_hbm, lw_hbm, act_hbm, gr_ref, gl_ref,
           xfull, cot, act, rg, lg, p1, p2, wt, lt, gracc, glacc,
           rsend, rrecv, lsend, lrecv,
           x_recv, x_send, x_local, c_local, a_out,
           rw_send, rw_recv, lw_send, lw_recv, gr_send, gr_recv, gl_send, gl_recv):
    d, p = lax.axis_index("dp"), lax.axis_index("mp")
    me = d * z.mp + p
    core = lax.rem(p, 2)
    partner = p + 1 - 2 * core
    chip = p // 2
    chips = z.mp // 2

    barrier = pltpu.get_barrier_semaphore()

    @pl.loop(1, z.n)
    def _(s):
        o = lax.rem(me + s, z.n)
        pl.semaphore_signal(barrier, inc=1, device_id=(o // z.mp, lax.rem(o, z.mp)), device_id_type=MESH)

    def rows(c):
        return pl.ds(pl.multiple_of(c * z.tc, z.tc), z.tc)

    def local_x(c):
        return pltpu.make_async_copy(x_hbm.at[rows(c)], xfull.at[p, rows(c)], x_local.at[c])

    def local_c(c):
        return pltpu.make_async_copy(cot_hbm.at[rows(c)], cot.at[rows(c)], c_local.at[c])

    def out_act(c):
        return pltpu.make_async_copy(act.at[rows(c)], act_hbm.at[rows(c)], a_out.at[c])

    def send_own(c, kind, target):
        return pltpu.make_async_remote_copy(
            src_ref=x_hbm.at[rows(c)], dst_ref=xfull.at[p, rows(c)],
            send_sem=x_send.at[kind, c], recv_sem=x_recv.at[p, c],
            device_id=(d, target), device_id_type=MESH)

    def forward(c, kind, source):
        return pltpu.make_async_remote_copy(
            src_ref=xfull.at[source, rows(c)], dst_ref=xfull.at[source, rows(c)],
            send_sem=x_send.at[kind, c], recv_sem=x_recv.at[source, c],
            device_id=(d, partner), device_id_type=MESH)

    def arrived(c, source):
        pltpu.make_async_remote_copy(
            src_ref=xfull.at[source, rows(c)], dst_ref=xfull.at[source, rows(c)],
            send_sem=x_send.at[0, c], recv_sem=x_recv.at[source, c],
            device_id=(d, partner), device_id_type=MESH).wait_recv()

    def same_core(s):
        return lax.rem(chip + s, chips) * 2 + core

    def other_core(s):
        return lax.rem(chip + s, chips) * 2 + 1 - core

    @pl.loop(0, CHUNKS)
    def _(c):
        local_x(c).start()
        local_c(c).start()

    pl.semaphore_wait(barrier, z.n - 1)

    own_rw = pltpu.make_async_copy(rw_hbm.at[p], rg.at[me], rw_recv)
    own_rw.start()
    own_lw = pltpu.make_async_copy(lw_hbm, lg.at[d], lw_recv)
    own_lw.start()

    @pl.loop(1, z.n)
    def _(s):
        o = lax.rem(me + s, z.n)
        q = lax.rem(o, z.mp)
        pltpu.make_async_remote_copy(
            src_ref=rw_hbm.at[q], dst_ref=rg.at[me], send_sem=rw_send, recv_sem=rw_recv,
            device_id=(o // z.mp, q), device_id_type=MESH).start()

    @pl.loop(1, z.dp)
    def _(s):
        pltpu.make_async_remote_copy(
            src_ref=lw_hbm, dst_ref=lg.at[d], send_sem=lw_send, recv_sem=lw_recv,
            device_id=(lax.rem(d + s, z.dp), p), device_id_type=MESH).start()

    @pl.loop(0, CHUNKS)
    def _(c):
        for s in range(1, chips):
            send_own(c, s, same_core(s)).start()
        send_own(c, 0, partner).start()

    for dd in range(z.dp):
        shape = (z.orow, z.feat)
        a, b = iota(shape, 0), iota(shape, 1)
        source = (b // z.bs) * z.rows + (b % z.bs) - dd * z.rows
        inside = (b % z.bs) // z.rows == dd
        p1[dd] = ones_where(inside & (a == source))
        shape = (z.orow, z.blocks * z.own)
        a, b = iota(shape, 0), iota(shape, 1)
        jg = b // z.rh
        i_all = (b % z.rh) // z.jl
        j = jg * z.jl + b % z.jl
        inside = i_all // z.rows == dd
        p2[dd] = ones_where(inside & (a == j * z.rows + i_all % z.rows))
    gracc[...] = jnp.zeros_like(gracc)
    glacc[...] = jnp.zeros_like(glacc)

    def count(ref, sem):
        pltpu.make_async_copy(ref, ref, sem).wait()

    count(lg, lw_recv)
    left = None
    for dd in range(z.dp):
        part = dot_nn(lg[dd], p2[dd])
        left = part if left is None else left + part
    left = left.astype(BF)
    shape = (z.fj, z.bs)
    spread = ones_where(iota(shape, 0) % z.bs == iota(shape, 1))
    for jg in range(z.jg):
        piece = dot_nn(spread, left[:, jg * z.rh:(jg + 1) * z.rh])
        keep = iota((z.fj, z.rh), 0) // z.bs == iota((z.fj, z.rh), 1) % z.jl
        lt[jg] = jnp.where(keep, piece, 0.0).astype(BF)

    count(rg, rw_recv)
    right = None
    for dd in range(z.dp):
        part = dot_nn(rg[dd * z.mp:(dd + 1) * z.mp].reshape(z.mp * z.pad, z.orow), p1[dd])
        right = part if right is None else right + part
    right = right.astype(BF)
    for g in range(z.groups):
        for s in range(z.gs):
            shape = (z.ng, z.mp * z.pad)
            a, b = iota(shape, 0), iota(shape, 1)
            j = (a // z.nj) * z.jl + a % z.jl
            src = (a % z.nj) // (z.own * z.jl)
            pick = ones_where((src == s) & (b == (g * z.gs + s) * z.pad + j))
            piece = dot_nn(pick, right)
            shape = (z.ng, z.feat)
            keep = (iota(shape, 0) // z.jl) % z.own == iota(shape, 1) // z.bs
            wt[g, :, s * z.feat:(s + 1) * z.feat] = jnp.where(keep, piece, 0.0).astype(BF)

    @pl.loop(0, CHUNKS)
    def _(c):
        local_x(c).wait()
        local_c(c).wait()
        for s in range(1, chips):
            arrived(c, same_core(s))
            forward(c, chips + s, same_core(s)).start()
        arrived(c, partner)
        for s in range(1, chips):
            arrived(c, other_core(s))
        r = rows(c)
        xs = [join([xfull[g * z.gs + s, r] for s in range(z.gs)]) for g in range(z.groups)]
        inner = [dot_nt(xs[g], wt[g]).astype(BF) for g in range(z.groups)]
        back = []
        for jg in range(z.jg):
            mixed = join([v[:, jg * z.nj:(jg + 1) * z.nj] for v in inner])
            pre = dot_nt(mixed, lt[jg])
            cdf = 0.5 * (1.0 + lax.erf(pre * 0.7071067811865476))
            slope = cdf + pre * (jnp.exp(-0.5 * pre * pre) * 0.3989422804014327)
            cols = pl.ds(jg * z.fj, z.fj)
            act[r, cols] = (pre * cdf).astype(BF)
            dpre = (cot[r, cols].astype(F32) * slope).astype(BF)
            glacc[jg] += dot_tn(dpre, mixed)
            back.append(dot_nn(dpre, lt[jg]).astype(BF))
        out_act(c).start()
        for g in range(z.groups):
            dinner = join([v[:, g * z.nj:(g + 1) * z.nj] for v in back])
            gracc[g] += dot_tn(dinner, xs[g])

    shape = (z.bs, z.fj)
    fold = ones_where(iota(shape, 1) % z.bs == iota(shape, 0))
    lefts = []
    for jg in range(z.jg):
        keep = iota((z.fj, z.rh), 0) // z.bs == iota((z.fj, z.rh), 1) % z.jl
        lefts.append(dot_nn(fold, jnp.where(keep, glacc[jg], 0.0).astype(BF)).astype(BF))
    left = join(lefts)
    for dd in range(z.dp):
        lsend[dd] = dot_nt(left, p2[dd]).astype(BF)

    @pl.loop(1, z.dp)
    def _(s):
        o = lax.rem(d + s, z.dp)
        pltpu.make_async_remote_copy(
            src_ref=lsend.at[o], dst_ref=lrecv.at[d], send_sem=gl_send, recv_sem=gl_recv,
            device_id=(o, p), device_id_type=MESH).start()

    for g in range(z.groups):
        for s in range(z.gs):
            shape = (z.pad, z.ng)
            a, b = iota(shape, 0), iota(shape, 1)
            j = (b // z.nj) * z.jl + b % z.jl
            src = (b % z.nj) // (z.own * z.jl)
            pick = ones_where((src == s) & (a == j))
            shape = (z.ng, z.feat)
            keep = (iota(shape, 0) // z.jl) % z.own == iota(shape, 1) // z.bs
            piece = jnp.where(keep, gracc[g, :, s * z.feat:(s + 1) * z.feat], 0.0).astype(BF)
            piece = dot_nn(pick, piece).astype(BF)
            for dd in range(z.dp):
                rsend[dd * z.mp + g * z.gs + s] = dot_nt(piece, p1[dd]).astype(BF)

    @pl.loop(1, z.n)
    def _(s):
        o = lax.rem(me + s, z.n)
        pltpu.make_async_remote_copy(
            src_ref=rsend.at[o], dst_ref=rrecv.at[me], send_sem=gr_send, recv_sem=gr_recv,
            device_id=(o // z.mp, lax.rem(o, z.mp)), device_id_type=MESH).start()

    lrecv[d] = lsend[d]
    rrecv[me] = rsend[me]

    @pl.loop(0, CHUNKS)
    def _(c):
        for s in range(1, chips):
            send_own(c, s, same_core(s)).wait_send()
            forward(c, chips + s, same_core(s)).wait_send()
        send_own(c, 0, partner).wait_send()
        out_act(c).wait()

    count(rg.at[pl.ds(0, z.n - 1)], rw_send)
    count(lg.at[pl.ds(0, z.dp - 1)], lw_send)

    count(lrecv.at[pl.ds(0, z.dp - 1)], gl_recv)
    total = lrecv[0].astype(F32)
    for dd in range(1, z.dp):
        total = total + lrecv[dd].astype(F32)
    gl_ref[...] = total
    count(rrecv.at[pl.ds(0, z.n - 1)], gr_recv)
    total = rrecv[0:z.mp].astype(F32)
    for dd in range(1, z.dp):
        total = total + rrecv[dd * z.mp:(dd + 1) * z.mp].astype(F32)
    gr_ref[...] = total
    count(lsend.at[pl.ds(0, z.dp - 1)], gl_send)
    count(rsend.at[pl.ds(0, z.n - 1)], gr_send)


def shards(z, tokens, right_weight, left_weight, cotangent):
    rw = right_weight.transpose(2, 0, 1).reshape(z.mp, z.own, z.orow)
    rw = jnp.pad(rw, ((0, 0), (0, z.pad - z.own), (0, 0)))
    lw = left_weight.transpose(2, 0, 1).reshape(z.bs, z.orow)
    hbm = pl.BlockSpec(memory_space=pltpu.HBM)
    vmem = pl.BlockSpec(memory_space=pltpu.VMEM)
    dma = pltpu.SemaphoreType.DMA
    act, gr, gl = pl.pallas_call(
        functools.partial(kernel, z),
        out_shape=(
            jax.ShapeDtypeStruct((z.tok, z.feat), BF),
            jax.ShapeDtypeStruct((z.mp, z.pad, z.orow), F32),
            jax.ShapeDtypeStruct((z.bs, z.orow), F32),
        ),
        in_specs=[hbm] * 4,
        out_specs=(hbm, vmem, vmem),
        scratch_shapes=[
            pltpu.VMEM((z.mp, z.tok, z.feat), BF),
            pltpu.VMEM((z.tok, z.feat), BF),
            pltpu.VMEM((z.tok, z.feat), BF),
            pltpu.VMEM((z.n, z.pad, z.orow), BF),
            pltpu.VMEM((z.dp, z.bs, z.orow), BF),
            pltpu.VMEM((z.dp, z.orow, z.feat), BF),
            pltpu.VMEM((z.dp, z.orow, z.blocks * z.own), BF),
            pltpu.VMEM((z.groups, z.ng, z.kg), BF),
            pltpu.VMEM((z.jg, z.fj, z.rh), BF),
            pltpu.VMEM((z.groups, z.ng, z.kg), F32),
            pltpu.VMEM((z.jg, z.fj, z.rh), F32),
            pltpu.VMEM((z.n, z.pad, z.orow), BF),
            pltpu.VMEM((z.n, z.pad, z.orow), BF),
            pltpu.VMEM((z.dp, z.bs, z.orow), BF),
            pltpu.VMEM((z.dp, z.bs, z.orow), BF),
            dma((z.mp, CHUNKS)),
            dma((z.mp, CHUNKS)),
            dma((CHUNKS,)),
            dma((CHUNKS,)),
            dma((CHUNKS,)),
            dma, dma, dma, dma, dma, dma, dma, dma,
        ],
        compiler_params=pltpu.CompilerParams(
            collective_id=0, has_side_effects=True, vmem_limit_bytes=60 * 1024 * 1024),
    )(tokens, cotangent, rw, lw)
    gr = gr[:, :z.own].reshape(z.mp * z.own, z.own, z.rows).transpose(1, 2, 0)
    gl = gl.reshape(z.bs, z.own, z.rows).transpose(1, 2, 0)
    return act, gr, gl


def solution(mesh):
    n_dp, n_mp = mesh.shape["dp"], mesh.shape["mp"]

    def step(tokens, right_weight, left_weight, cotangent):
        z = Sizes(n_dp, n_mp, tokens.shape[0] // n_dp, tokens.shape[1] // n_mp, right_weight.shape[1])
        return jax.shard_map(
            functools.partial(shards, z),
            mesh=mesh,
            in_specs=(P("dp", "mp"), P("mp", "dp", None), P("mp", "dp", None), P("dp", "mp")),
            out_specs=(P("dp", "mp"), P("mp", "dp", None), P("mp", "dp", None)),
            check_vma=False,
        )(tokens, right_weight, left_weight, cotangent)

    return step
```

time: 237 us -> 79.2 us (0.33)
  waiting for transfers between devices: 120 us -> 0 us
  Pallas kernels: 0 us -> 68.9 us
  blocking collectives: 55 us -> 0 us
  matrix products: 21.9 us -> 0 us
  between operations: 14.1 us -> 0.65 us
  starting transfers between devices: 8.99 us -> 0 us
  local copies, waits for them, and re-layouts: 15.9 us -> 9.27 us
    reduce_scatter x2 -> x0, waiting for transfers between devices: 98.6 us -> none  [the longest x1 66.1 us: shards(): lax.psum_scatter(part_right, 'dp', scatter_dimension=1, tiled=True)]
    pallas_call x0 -> x1, Pallas kernels: none -> 68.9 us  [shards(): pl.pallas_call(functools.partial(kernel, z), out_shape=(jax.ShapeDtypeStr...]
    all_gather x2 -> x0, blocking collectives: 55 us -> none  [the longest x1 28.6 us: shards(): lax.all_gather(right_weight, 'dp', axis=1, tiled=True)]
    dot_general x5 -> x0, matrix products: 21.9 us -> none  [the longest x1 13.7 us: shards(): jnp.einsum('tpmj,mpjn->tmn', mixed, left_four, preferred_element_type=jnp...]
    all_to_all x2 -> x0, waiting for transfers between devices: 21.9 us -> none  [the longest x1 21.9 us: shards(): lax.all_to_all(dmixed, 'mp', split_axis=1, concat_axis=1, tiled=True)]
    all_to_all x2 -> x0, starting transfers between devices: 8.91 us -> none  [the longest x1 4.47 us: shards(): lax.all_to_all(inner, 'mp', split_axis=1, concat_axis=1, tiled=True)]
    convert_element_type x3 -> x0, local copies, waits for them, and re-layouts: 8.1 us -> none  [the longest x1 4.13 us: shards(): cotangent.reshape(tok_rows, owned, BS).astype(jnp.float32) * gelu_slope(pre)]
    unnamed x6 -> x1, local copies, waits for them, and re-layouts: 6.83 us -> 3.08 us
  transfers between devices with their start and end apart: 4 -> 0, of which waited for: 3 -> 0; matrix products, arithmetic and copies ran while one was open for 7% -> 0% of each run, Pallas kernels for 0% -> 0%
where the time goes in v1:
time: 79.2 us; the launch traced here: 78.8 us
  Pallas kernels  68.9 us (87%)
  local copies, waits for them, and re-layouts  9.27 us (12%)
    pallas_call x1, Pallas kernels, shards(): pl.pallas_call(functools.partial(kernel, z), out_shape=(jax.ShapeDtypeStr...  68.9 us
    unnamed x1, local copies, waits for them, and re-layouts  3.08 us
    pallas_call x2, local copies, waits for them, and re-layouts, shards(): pl.pallas_call(functools.partial(kernel, z), out_shape=(jax.ShapeDtypeStr...  2.39 us

profile of v1, /device:TPU:0, one launch (start us, length us, event | category | flops | bytes accessed | tf_op | source)
XLA Modules:
  0.0 78.8 jit_solution(2894838085679327835)
XLA Ops:
  0.6 1.4 %copy.12.lw_hbm = bf16[64,128]{1,0:T(8,128)(2,1)} copy(bf16[64,128]{0,1:T(8,128)(2,1)} %bitcast.15) | data formatting | bytes 32768 | tf_op jit(solution)/shard_map/reshape | solution.py:297
  2.1 0.9 %reshape.18 = bf16[4,16,128]{1,0,2:T(4,128)(2,1)S(1)} reshape(bf16[64,16,8]{0,2,1:T(8,128)(2,1)} %bitcast.14) | data formatting | bytes 32768 | tf_op jit(solution)/shard_map/reshape | solution.py:295
  3.0 0.7 copy.11.rw_hbm
  3.7 68.9 %shard_map.67 = (bf16[1024,1024]{1,0:T(8,128)(2,1)}, f32[4,16,128]{2,1,0:T(8,128)}, f32[64,128]{1,0:T(8,128)}) custom-call(bf16[1024,1024]{1,0:T(8,128)(2,1)} %x_hbm.1, bf16[1024,1024]{1,0:T(8,128)(2,1)} %cot_hbm.1, bf16[4,16,128]{2,1,0:T(8,128)(2,1)} %copy.11.rw_hbm, bf16[64,128]{1,0:T(8,128)(2,1)} %copy.12.lw_hbm), custom_call_target="tpu_custom_call" | custom-call | tf_op jit(solution)/shard_map/pallas_call | solution.py:301
  72.5 1.5 %copy.14 = f32[64,128]{0,1:T(8,128)} copy(f32[64,128]{1,0:T(8,128)} %get-tuple-element.8) | data formatting | bytes 65536 | tf_op jit(solution)/shard_map/pallas_call | solution.py:301
  74.0 0.9 %copy.13 = f32[4,16,128]{1,0,2:T(4,128)S(1)} copy(f32[4,16,128]{2,1,0:T(8,128)} %get-tuple-element.7) | data formatting | bytes 65536 | tf_op jit(solution)/shard_map/pallas_call | solution.py:301
  74.9 0.8 %reshape.20 = f32[64,16,8]{0,2,1:T(8,128)} reshape(f32[4,16,128]{1,0,2:T(4,128)S(1)} %copy.13) | data formatting | bytes 65536 | tf_op jit(solution)/shard_map/reshape | solution.py:336
  75.7 3.1 %copy.16 = bf16[1024,1024]{1,0:T(8,128)(2,1)} copy(bf16[1024,1024]{1,0:T(8,128)(2,1)} %get-tuple-element.12) | data formatting | bytes 4194304

commit v2 on v1

--- a/solution.py
+++ b/solution.py
@@ -14,7 +14,8 @@
 
 
 def iota(shape, dim):
-    return lax.broadcasted_iota(jnp.int32, shape, dim)
+    line = tuple(n if axis == dim else 1 for axis, n in enumerate(shape))
+    return lax.broadcasted_iota(jnp.int32, line, dim)
 
 
 def ones_where(cond):
@@ -56,13 +57,14 @@
         self.rh = self.groups * self.nj
         self.fj = self.jl * width
         self.n = n_dp * n_mp
+        self.direct = self.pad == self.own and self.orow % 128 == 0
         self.tc = tok_rows // CHUNKS
 
 
 def kernel(z, x_hbm, cot_hbm, rw_hbm, lw_hbm, act_hbm, gr_ref, gl_ref,
-           xfull, cot, act, rg, lg, p1, p2, wt, lt, gracc, glacc,
+           xfull, cot, act, rw_v, lw_v, rwt, lwt, rg, lg, p1, p2, wt, lt, gracc, glacc,
            rsend, rrecv, lsend, lrecv,
-           x_recv, x_send, x_local, c_local, a_out,
+           x_recv, x_send, x_local, c_local, a_out, w_local,
            rw_send, rw_recv, lw_send, lw_recv, gr_send, gr_recv, gl_send, gl_recv):
     d, p = lax.axis_index("dp"), lax.axis_index("mp")
     me = d * z.mp + p
@@ -119,32 +121,47 @@
         local_x(c).start()
         local_c(c).start()
 
+    local_r = pltpu.make_async_copy(rw_hbm, rw_v, w_local.at[0])
+    local_r.start()
+    local_l = pltpu.make_async_copy(lw_hbm, lw_v, w_local.at[1])
+    local_l.start()
+    local_r.wait()
+    local_l.wait()
+    shape = (z.mp * z.pad, z.bs)
+    a, b = iota(shape, 0), iota(shape, 1)
+    wide = ones_where((a % z.pad < z.own) & (b == (a // z.pad) * z.own + a % z.pad))
+    rwt[...] = dot_nt(wide, rw_v[...]).astype(BF).reshape(z.mp, z.pad, z.orow)
+    shape = (z.bs, z.bs)
+    lwt[...] = dot_nt(ones_where(iota(shape, 0) == iota(shape, 1)), lw_v[...]).astype(BF)
+    rg[me] = rwt[p]
+    lg[d] = lwt[...]
+
     pl.semaphore_wait(barrier, z.n - 1)
 
-    own_rw = pltpu.make_async_copy(rw_hbm.at[p], rg.at[me], rw_recv)
-    own_rw.start()
-    own_lw = pltpu.make_async_copy(lw_hbm, lg.at[d], lw_recv)
-    own_lw.start()
-
-    @pl.loop(1, z.n)
-    def _(s):
-        o = lax.rem(me + s, z.n)
-        q = lax.rem(o, z.mp)
-        pltpu.make_async_remote_copy(
-            src_ref=rw_hbm.at[q], dst_ref=rg.at[me], send_sem=rw_send, recv_sem=rw_recv,
-            device_id=(o // z.mp, q), device_id_type=MESH).start()
-
-    @pl.loop(1, z.dp)
-    def _(s):
-        pltpu.make_async_remote_copy(
-            src_ref=lw_hbm, dst_ref=lg.at[d], send_sem=lw_send, recv_sem=lw_recv,
-            device_id=(lax.rem(d + s, z.dp), p), device_id_type=MESH).start()
-
-    @pl.loop(0, CHUNKS)
-    def _(c):
+    def send_x(c):
         for s in range(1, chips):
             send_own(c, s, same_core(s)).start()
         send_own(c, 0, partner).start()
+
+    send_x(0)
+
+    @pl.loop(1, z.n)
+    def _(s):
+        o = lax.rem(me + s, z.n)
+        q = lax.rem(o, z.mp)
+        pltpu.make_async_remote_copy(
+            src_ref=rwt.at[q], dst_ref=rg.at[me], send_sem=rw_send, recv_sem=rw_recv,
+            device_id=(o // z.mp, q), device_id_type=MESH).start()
+
+    @pl.loop(1, z.dp)
+    def _(s):
+        pltpu.make_async_remote_copy(
+            src_ref=lwt, dst_ref=lg.at[d], send_sem=lw_send, recv_sem=lw_recv,
+            device_id=(lax.rem(d + s, z.dp), p), device_id_type=MESH).start()
+
+    @pl.loop(1, CHUNKS)
+    def _(c):
+        send_x(c)
 
     for dd in range(z.dp):
         shape = (z.orow, z.feat)
@@ -165,7 +182,7 @@
     def count(ref, sem):
         pltpu.make_async_copy(ref, ref, sem).wait()
 
-    count(lg, lw_recv)
+    count(lg.at[pl.ds(0, z.dp - 1)], lw_recv)
     left = None
     for dd in range(z.dp):
         part = dot_nn(lg[dd], p2[dd])
@@ -178,7 +195,7 @@
         keep = iota((z.fj, z.rh), 0) // z.bs == iota((z.fj, z.rh), 1) % z.jl
         lt[jg] = jnp.where(keep, piece, 0.0).astype(BF)
 
-    count(rg, rw_recv)
+    count(rg.at[pl.ds(0, z.n - 1)], rw_recv)
     right = None
     for dd in range(z.dp):
         part = dot_nn(rg[dd * z.mp:(dd + 1) * z.mp].reshape(z.mp * z.pad, z.orow), p1[dd])
@@ -242,6 +259,7 @@
             src_ref=lsend.at[o], dst_ref=lrecv.at[d], send_sem=gl_send, recv_sem=gl_recv,
             device_id=(o, p), device_id_type=MESH).start()
 
+    pieces = []
     for g in range(z.groups):
         for s in range(z.gs):
             shape = (z.pad, z.ng)
@@ -252,9 +270,11 @@
             shape = (z.ng, z.feat)
             keep = (iota(shape, 0) // z.jl) % z.own == iota(shape, 1) // z.bs
             piece = jnp.where(keep, gracc[g, :, s * z.feat:(s + 1) * z.feat], 0.0).astype(BF)
-            piece = dot_nn(pick, piece).astype(BF)
-            for dd in range(z.dp):
-                rsend[dd * z.mp + g * z.gs + s] = dot_nt(piece, p1[dd]).astype(BF)
+            pieces.append(dot_nn(pick, piece).astype(BF))
+    pieces = join(pieces, axis=0)
+    for dd in range(z.dp):
+        owned = dot_nt(pieces, p1[dd]).astype(BF)
+        rsend[dd * z.mp:(dd + 1) * z.mp] = owned.reshape(z.mp, z.pad, z.orow)
 
     @pl.loop(1, z.n)
     def _(s):
@@ -281,20 +301,19 @@
     total = lrecv[0].astype(F32)
     for dd in range(1, z.dp):
         total = total + lrecv[dd].astype(F32)
-    gl_ref[...] = total
+    gl_ref[...] = total.T if z.direct else total
     count(rrecv.at[pl.ds(0, z.n - 1)], gr_recv)
     total = rrecv[0:z.mp].astype(F32)
     for dd in range(1, z.dp):
         total = total + rrecv[dd * z.mp:(dd + 1) * z.mp].astype(F32)
-    gr_ref[...] = total
+    gr_ref[...] = total.reshape(z.blocks, z.orow).T if z.direct else total
     count(lsend.at[pl.ds(0, z.dp - 1)], gl_send)
     count(rsend.at[pl.ds(0, z.n - 1)], gr_send)
 
 
 def shards(z, tokens, right_weight, left_weight, cotangent):
-    rw = right_weight.transpose(2, 0, 1).reshape(z.mp, z.own, z.orow)
-    rw = jnp.pad(rw, ((0, 0), (0, z.pad - z.own), (0, 0)))
-    lw = left_weight.transpose(2, 0, 1).reshape(z.bs, z.orow)
+    rw = right_weight.reshape(z.orow, z.bs)
+    lw = left_weight.reshape(z.orow, z.bs)
     hbm = pl.BlockSpec(memory_space=pltpu.HBM)
     vmem = pl.BlockSpec(memory_space=pltpu.VMEM)
     dma = pltpu.SemaphoreType.DMA
@@ -302,8 +321,8 @@
         functools.partial(kernel, z),
         out_shape=(
             jax.ShapeDtypeStruct((z.tok, z.feat), BF),
-            jax.ShapeDtypeStruct((z.mp, z.pad, z.orow), F32),
-            jax.ShapeDtypeStruct((z.bs, z.orow), F32),
+            jax.ShapeDtypeStruct((z.orow, z.bs) if z.direct else (z.mp, z.pad, z.orow), F32),
+            jax.ShapeDtypeStruct((z.orow, z.bs) if z.direct else (z.bs, z.orow), F32),
         ),
         in_specs=[hbm] * 4,
         out_specs=(hbm, vmem, vmem),
@@ -311,6 +330,10 @@
             pltpu.VMEM((z.mp, z.tok, z.feat), BF),
             pltpu.VMEM((z.tok, z.feat), BF),
             pltpu.VMEM((z.tok, z.feat), BF),
+            pltpu.VMEM((z.orow, z.bs), BF),
+            pltpu.VMEM((z.orow, z.bs), BF),
+            pltpu.VMEM((z.mp, z.pad, z.orow), BF),
+            pltpu.VMEM((z.bs, z.orow), BF),
             pltpu.VMEM((z.n, z.pad, z.orow), BF),
             pltpu.VMEM((z.dp, z.bs, z.orow), BF),
             pltpu.VMEM((z.dp, z.orow, z.feat), BF),
@@ -328,11 +351,14 @@
             dma((CHUNKS,)),
             dma((CHUNKS,)),
             dma((CHUNKS,)),
+            dma((2,)),
             dma, dma, dma, dma, dma, dma, dma, dma,
         ],
         compiler_params=pltpu.CompilerParams(
             collective_id=0, has_side_effects=True, vmem_limit_bytes=60 * 1024 * 1024),
     )(tokens, cotangent, rw, lw)
+    if z.direct:
+        return act, gr.reshape(z.own, z.rows, z.bs), gl.reshape(z.own, z.rows, z.bs)
     gr = gr[:, :z.own].reshape(z.mp * z.own, z.own, z.rows).transpose(1, 2, 0)
     gl = gl.reshape(z.bs, z.own, z.rows).transpose(1, 2, 0)
     return act, gr, gl

time: 79.2 us -> 74.3 us (0.938)
  local copies, waits for them, and re-layouts: 9.27 us -> 4.38 us
    reshape x4 -> x0, local copies, waits for them, and re-layouts: 3.81 us -> none  [the longest x2 1.57 us: shards(): rw = right_weight.transpose(2, 0, 1).reshape(z.mp, z.own, z.orow)]
    pallas_call x2 -> x0, local copies, waits for them, and re-layouts: 2.39 us -> none  [shards(): pl.pallas_call(functools.partial(kernel, z), out_shape=(jax.ShapeDtypeStr...]
    unnamed x1 -> x7, local copies, waits for them, and re-layouts: 3.08 us -> 4.38 us
where the time goes in v2:
time: 74.3 us; the launch traced here: 74.1 us
  Pallas kernels  69.1 us (93%)
  local copies, waits for them, and re-layouts  4.38 us (6%)
    pallas_call x1, Pallas kernels, shards(): pl.pallas_call(functools.partial(kernel, z), out_shape=(jax.ShapeDtypeStr...  69.1 us
    unnamed x7, local copies, waits for them, and re-layouts  4.38 us

profile of v2, /device:TPU:0, one launch (start us, length us, event | category | flops | bytes accessed | tf_op | source)
XLA Modules:
  0.0 74.1 jit_solution(1318038791359777240)
XLA Ops:
  0.6 69.1 %shard_map.67 = (bf16[1024,1024]{1,0:T(8,128)(2,1)}, f32[128,64]{1,0:T(8,128)}, f32[128,64]{1,0:T(8,128)}) custom-call(bf16[1024,1024]{1,0:T(8,128)(2,1)} %x_hbm.1, bf16[1024,1024]{1,0:T(8,128)(2,1)} %cot_hbm.1, bf16[128,64]{1,0:T(8,128)(2,1)} %bitcast.6, bf16[128,64]{1,0:T(8,128)(2,1)} %bitcast.7), custom_call_target="tpu_custom_call" | custom-call | tf_op jit(solution)/shard_map/pallas_call | solution.py:320
  69.7 0.0 copy-start.1
  69.7 0.0 copy-start
  69.7 3.1 %copy.10 = bf16[1024,1024]{1,0:T(8,128)(2,1)} copy(bf16[1024,1024]{1,0:T(8,128)(2,1)} %get-tuple-element.12) | data formatting | bytes 4194304
  72.8 0.0 copy-done.1
  72.8 0.6 copy.11
  73.5 0.0 copy-done
  73.5 0.6 copy.12
Async XLA Ops:
  69.7 3.1 %copy-start.1 = (f32[128,64]{1,0:T(8,128)S(1)}, f32[128,64]{1,0:T(8,128)}, u32[]{:S(2)}) copy-start(f32[128,64]{1,0:T(8,128)} %get-tuple-element.7) | copy-start | bytes 98308
  69.7 3.8 %copy-start = (f32[128,64]{1,0:T(8,128)S(1)}, f32[128,64]{1,0:T(8,128)}, u32[]{:S(2)}) copy-start(f32[128,64]{1,0:T(8,128)} %get-tuple-element.8) | copy-start | bytes 98308

commit v3 on v2

--- a/solution.py
+++ b/solution.py
@@ -61,10 +61,10 @@
         self.tc = tok_rows // CHUNKS
 
 
-def kernel(z, x_hbm, cot_hbm, rw_hbm, lw_hbm, act_hbm, gr_ref, gl_ref,
-           xfull, cot, act, rw_v, lw_v, rwt, lwt, rg, lg, p1, p2, wt, lt, gracc, glacc,
+def kernel(z, x_hbm, cot_hbm, rw_hbm, lw_hbm, act, gr_ref, gl_ref,
+           xfull, cot, rw_v, lw_v, rwt, lwt, rg, lg, p1, p2, wt, lt, gracc, glacc,
            rsend, rrecv, lsend, lrecv,
-           x_recv, x_send, x_local, c_local, a_out, w_local,
+           x_recv, x_send, x_local, c_local, w_local,
            rw_send, rw_recv, lw_send, lw_recv, gr_send, gr_recv, gl_send, gl_recv):
     d, p = lax.axis_index("dp"), lax.axis_index("mp")
     me = d * z.mp + p
@@ -88,9 +88,6 @@
 
     def local_c(c):
         return pltpu.make_async_copy(cot_hbm.at[rows(c)], cot.at[rows(c)], c_local.at[c])
-
-    def out_act(c):
-        return pltpu.make_async_copy(act.at[rows(c)], act_hbm.at[rows(c)], a_out.at[c])
 
     def send_own(c, kind, target):
         return pltpu.make_async_remote_copy(
@@ -237,7 +234,6 @@
             dpre = (cot[r, cols].astype(F32) * slope).astype(BF)
             glacc[jg] += dot_tn(dpre, mixed)
             back.append(dot_nn(dpre, lt[jg]).astype(BF))
-        out_act(c).start()
         for g in range(z.groups):
             dinner = join([v[:, g * z.nj:(g + 1) * z.nj] for v in back])
             gracc[g] += dot_tn(dinner, xs[g])
@@ -292,7 +288,6 @@
             send_own(c, s, same_core(s)).wait_send()
             forward(c, chips + s, same_core(s)).wait_send()
         send_own(c, 0, partner).wait_send()
-        out_act(c).wait()
 
     count(rg.at[pl.ds(0, z.n - 1)], rw_send)
     count(lg.at[pl.ds(0, z.dp - 1)], lw_send)
@@ -320,15 +315,14 @@
     act, gr, gl = pl.pallas_call(
         functools.partial(kernel, z),
         out_shape=(
-            jax.ShapeDtypeStruct((z.tok, z.feat), BF),
+            pltpu.VMEM((z.tok, z.feat), BF),
             jax.ShapeDtypeStruct((z.orow, z.bs) if z.direct else (z.mp, z.pad, z.orow), F32),
             jax.ShapeDtypeStruct((z.orow, z.bs) if z.direct else (z.bs, z.orow), F32),
         ),
         in_specs=[hbm] * 4,
-        out_specs=(hbm, vmem, vmem),
+        out_specs=(vmem, vmem, vmem),
         scratch_shapes=[
             pltpu.VMEM((z.mp, z.tok, z.feat), BF),
-            pltpu.VMEM((z.tok, z.feat), BF),
             pltpu.VMEM((z.tok, z.feat), BF),
             pltpu.VMEM((z.orow, z.bs), BF),
             pltpu.VMEM((z.orow, z.bs), BF),
@@ -350,12 +344,11 @@
             dma((z.mp, CHUNKS)),
             dma((CHUNKS,)),
             dma((CHUNKS,)),
-            dma((CHUNKS,)),
             dma((2,)),
             dma, dma, dma, dma, dma, dma, dma, dma,
         ],
         compiler_params=pltpu.CompilerParams(
-            collective_id=0, has_side_effects=True, vmem_limit_bytes=60 * 1024 * 1024),
+            collective_id=0, has_side_effects=True, vmem_limit_bytes=61 * 1024 * 1024),
     )(tokens, cotangent, rw, lw)
     if z.direct:
         return act, gr.reshape(z.own, z.rows, z.bs), gl.reshape(z.own, z.rows, z.bs)

time: 74.3 us -> 72.4 us (0.974)
  local copies, waits for them, and re-layouts: 4.38 us -> 2.59 us
    unnamed x7, local copies, waits for them, and re-layouts: 4.38 us -> 2.59 us
where the time goes in v3:
time: 72.4 us; the launch traced here: 72.2 us
  Pallas kernels  69 us (95%)
  local copies, waits for them, and re-layouts  2.59 us (4%)
    pallas_call x1, Pallas kernels, shards(): pl.pallas_call(functools.partial(kernel, z), out_shape=(pltpu.VMEM((z.tok...  69 us
    unnamed x7, local copies, waits for them, and re-layouts  2.59 us

profile of v3, /device:TPU:0, one launch (start us, length us, event | category | flops | bytes accessed | tf_op | source)
XLA Modules:
  0.0 72.2 jit_solution(4714712684108868352)
XLA Ops:
  0.6 69.0 %shard_map.67 = (bf16[1024,1024]{1,0:T(8,128)(2,1)S(1)}, f32[128,64]{1,0:T(8,128)}, f32[128,64]{1,0:T(8,128)}) custom-call(bf16[1024,1024]{1,0:T(8,128)(2,1)} %x_hbm.1, bf16[1024,1024]{1,0:T(8,128)(2,1)} %cot_hbm.1, bf16[128,64]{1,0:T(8,128)(2,1)} %bitcast.6, bf16[128,64]{1,0:T(8,128)(2,1)} %bitcast.7), custom_call_target="tpu_custom_call" | custom-call | tf_op jit(solution)/shard_map/pallas_call | solution.py:315
  69.6 0.0 copy-start.1
  69.6 0.0 copy-start
  69.6 1.3 %copy.10 = bf16[1024,1024]{1,0:T(8,128)(2,1)} copy(bf16[1024,1024]{1,0:T(8,128)(2,1)S(1)} %get-tuple-element.9) | data formatting | bytes 4194304
  71.0 0.0 copy-done.1
  71.0 0.6 copy.11
  71.6 0.0 copy-done
  71.6 0.6 copy.12
Async XLA Ops:
  69.6 1.3 %copy-start.1 = (f32[128,64]{1,0:T(8,128)S(1)}, f32[128,64]{1,0:T(8,128)}, u32[]{:S(2)}) copy-start(f32[128,64]{1,0:T(8,128)} %get-tuple-element.7) | copy-start | bytes 98308
  69.6 2.0 %copy-start = (f32[128,64]{1,0:T(8,128)S(1)}, f32[128,64]{1,0:T(8,128)}, u32[]{:S(2)}) copy-start(f32[128,64]{1,0:T(8,128)} %get-tuple-element.8) | copy-start | bytes 98308
